TPU v7x, 32 devices: a whole 2x2x4 slice. The times are simulated.
32 devices in a mesh: groups: 2 (over x), dp: 4 (over y, core), fsdp: 4 (over z).
Axes of the slice: x: 2, y: 2, z: 4, core: 2. Of those that a mesh axis runs over, the one named last changes fastest.
Arguments:
- tokens: bfloat16 [4096, 4096], P(('groups', 'dp', 'fsdp')), parts along dimension 0, may hold values from -6 to 6
- up_weight: bfloat16 [4096, 14336], P('fsdp', 'dp'), may hold values from -0.09375 to 0.09375
- first_adapter_factors: bfloat16 [32, 32, 4096], P(('groups', 'dp', 'fsdp')), parts along dimension 0, may hold values from -0.09375 to 0.09375
- second_adapter_factors: bfloat16 [32, 32, 14336], P(('groups', 'dp', 'fsdp')), parts along dimension 0, may hold values from -1 to 1
- counts: int32 [32], P(('groups', 'dp', 'fsdp')), parts along dimension 0, may hold values from 1 to 128, as said below
- output_gradient: bfloat16 [4096, 14336], P(('groups', 'dp', 'fsdp')), parts along dimension 0, may hold values from -6 to 6
Outputs:
- act_out: bfloat16 [4096, 14336], P(('groups', 'dp', 'fsdp')), parts along dimension 0
- grad_a: float32 [32, 32, 4096], P(('groups', 'dp', 'fsdp')), parts along dimension 0
- second_factor_gradient: float32 [32, 32, 14336], P(('groups', 'dp', 'fsdp')), parts along dimension 0
There are 2 independent parts, one for each index of `groups`. A program takes and returns all parts, laid end to end along the dimension named above; an argument that names none is the same for every part. Nothing has to cross between parts.
Inputs may be any that keep to these rules, and one draw needn't show every extreme that they name: counts[d] is the number of live rows of adapter d. For d < 8, counts[d] + counts[d + 8] <= 160; in every draw some such pair has the counts 128 and 32.
All inputs are finite; a program needn't handle non-finite values.
Results may differ from a plain program's by a relative error of at most 0.0058.
Values may be sent and summed in bfloat16 or wider, within the bound.
No kernel may reach another device: no remote copies, remote signals or barrier semaphores. Data moves between devices by JAX's collectives and lax.ppermute only.
A program may use at most 128 MiB of HBM per device.

v0:
```python
import jax
import jax.numpy as jnp
from jax import lax
from jax.sharding import PartitionSpec as P

SLOTS = 128
PAIR_ROWS = 80
LOWRANK_SCALE = 2.0


def partner(x, axis, distance):
    return lax.ppermute(x, axis, [(i, i ^ 1 << distance) for i in range(lax.axis_size(axis))])


def silu_slope(inputs):
    gate_value = jax.nn.sigmoid(inputs)
    return gate_value * (1.0 + inputs * (1.0 - gate_value))


def take_block(rows_all, offset, row_count):
    filler = jnp.zeros((row_count,) + rows_all.shape[1:], rows_all.dtype)
    padded = jnp.concatenate([rows_all, filler], 0)
    return lax.dynamic_slice_in_dim(padded, offset, row_count, 0)


def place_block(rows_kept, block, offset, row_total):
    filler = jnp.zeros((block.shape[0],) + rows_kept.shape[1:], rows_kept.dtype)
    padded = jnp.concatenate([rows_kept, filler], 0)
    placed = lax.dynamic_update_slice_in_dim(padded, block, offset, 0)
    return placed[:row_total]


def per_device(
    tokens, up_weight, first_adapter_factors, second_adapter_factors, counts, output_gradient
):
    down_factor = first_adapter_factors[0]
    up_factor = second_adapter_factors[0]
    slot_total = tokens.shape[0]
    own_count = counts[0]
    live_rows = jnp.arange(slot_total, dtype=jnp.int32)[:, None] < own_count
    spare_rows = SLOTS - PAIR_ROWS
    half_bit = lax.axis_size("dp").bit_length() - 2
    kept_rows = jnp.minimum(own_count, PAIR_ROWS)
    outgoing = take_block(tokens, kept_rows, spare_rows)
    guest = partner(outgoing, "dp", half_bit)
    paired_rows = place_block(tokens[:PAIR_ROWS], guest, kept_rows, PAIR_ROWS)
    dp_total, fsdp_total = (lax.axis_size("dp"), lax.axis_size("fsdp"))
    sliced_rows = lax.all_to_all(paired_rows, "fsdp", split_axis=1, concat_axis=0, tiled=True)
    slice_width = sliced_rows.shape[1]
    all_rows = lax.all_gather(sliced_rows, "dp", axis=0, tiled=True)
    all_rows = all_rows.reshape(dp_total, fsdp_total, PAIR_ROWS, slice_width).swapaxes(0, 1)
    partial_blocks = jnp.dot(
        all_rows.reshape(-1, slice_width), up_weight, preferred_element_type=jnp.float32
    ).astype(jnp.bfloat16)
    blocks = lax.psum_scatter(partial_blocks, "fsdp", scatter_dimension=0, tiled=True)
    paired_base = lax.all_to_all(blocks, "dp", split_axis=0, concat_axis=1, tiled=True)
    returned = partner(take_block(paired_base, kept_rows, spare_rows), "dp", half_bit)
    base_output = place_block(paired_base, returned, kept_rows, SLOTS)
    rank_projection = lax.dot_general(
        tokens, down_factor, (((1,), (1,)), ((), ())), preferred_element_type=jnp.float32
    ).astype(jnp.bfloat16)
    adapter_update = jnp.dot(rank_projection, up_factor, preferred_element_type=jnp.float32)
    hidden_preactivation = base_output.astype(jnp.float32) + LOWRANK_SCALE * adapter_update
    act_out = jnp.where(live_rows, jax.nn.silu(hidden_preactivation), 0.0).astype(jnp.bfloat16)
    grad_pre = jnp.where(
        live_rows, output_gradient.astype(jnp.float32) * silu_slope(hidden_preactivation), 0.0
    ).astype(jnp.bfloat16)
    low_rank_gradient = (
        LOWRANK_SCALE
        * lax.dot_general(
            grad_pre, up_factor, (((1,), (1,)), ((), ())), preferred_element_type=jnp.float32
        )
    ).astype(jnp.bfloat16)
    second_factor_gradient = LOWRANK_SCALE * lax.dot_general(
        rank_projection, grad_pre, (((0,), (0,)), ((), ())), preferred_element_type=jnp.float32
    )
    grad_a = lax.dot_general(
        low_rank_gradient, tokens, (((0,), (0,)), ((), ())), preferred_element_type=jnp.float32
    )
    return (act_out, grad_a[None], second_factor_gradient[None])


def solution(mesh):
    placed = (
        P(("groups", "dp", "fsdp"), None),
        P("fsdp", "dp"),
        P(("groups", "dp", "fsdp"), None, None),
        P(("groups", "dp", "fsdp"), None, None),
        P(("groups", "dp", "fsdp")),
        P(("groups", "dp", "fsdp"), None),
    )
    return jax.shard_map(
        per_device,
        mesh=mesh,
        in_specs=placed,
        out_specs=(
            P(("groups", "dp", "fsdp"), None),
            P(("groups", "dp", "fsdp"), None, None),
            P(("groups", "dp", "fsdp"), None, None),
        ),
        check_vma=False,
    )
```

profile of v0, /device:TPU:0, one launch (start us, length us, event | category | flops | bytes accessed | tf_op | source)
XLA Modules:
  0.0 340.4 jit_solution(10477999457115856074)
XLA Ops:
  7.2 0.0 copy-start
  7.2 0.0 all-gather.2.cloned.1.call-start
  8.0 1.2 pad_dynamic-slice_fusion
  9.1 3.1 collective-permute-start
  12.2 1.4 broadcast_select_fusion
  13.6 7.7 %collective-permute-done = bf16[48,4096]{1,0:T(8,128)(2,1)S(1)} collective-permute-done((bf16[48,4096]{1,0:T(8,128)(2,1)S(1)}, bf16[48,4096]{1,0:T(8,128)(2,1)S(1)}, u32[]{:S(2)}, u32[]{:S(2)}) %collective-permute-start) | collective-permute-done | bytes 393248 | tf_op jit(solution)/shard_map/ppermute | solution.py:12
  21.3 2.3 dynamic_update_slice.6
  23.6 21.0 %all_to_all.38 = bf16[80,4,1024]{2,0,1:T(8,128)(2,1)} all-to-all(bf16[80,4,1024]{2,0,1:T(8,128)(2,1)S(1)} %bitcast.49), channel_id=1, replica_groups=mesh['groups'=2,'dp'=4,'fsdp'=4] {'fsdp'}, dimensions={1} | all-to-all | bytes 1310720 | tf_op jit(solution)/shard_map/all_to_all | solution.py:48
  44.7 0.0 all-gather.2.cloned.1.call-update
  44.7 0.0 reduce-scatter.2.cloned.1.call-start
  44.7 25.2 %all-gather.2.cloned.1.call-done = bf16[1280,1024]{1,0:T(8,128)(2,1)} async-done(((bf16[320,1024]{1,0:T(8,128)(2,1)}), bf16[1280,1024]{1,0:T(8,128)(2,1)}) %all-gather.2.cloned.1.call-update) | async-done | bytes 2621456 | tf_op jit(solution)/shard_map/all_gather | solution.py:50
  69.9 2.1 copy.16
  72.0 14.9 %convolution_convert_fusion = bf16[1280,3584]{1,0:T(8,128)(2,1)} fusion(bf16[1280,1024]{1,0:T(8,128)(2,1)S(1)} %bitcast.46, bf16[1024,3584]{1,0:T(8,128)(2,1)} %param.7), kind=kOutput, calls=%fused_computation.3 | convolution fusion | flops 9399828480 | bytes 19136512 | tf_op jit(solution)/shard_map/dot_general | solution.py:52
  86.9 0.0 reduce-scatter.2.cloned.1.call-update
  86.9 157.2 %reduce-scatter.2.cloned.1.call-done = bf16[320,3584]{1,0:T(8,128)(2,1)} async-done(((bf16[1280,3584]{1,0:T(8,128)(2,1)}), bf16[320,3584]{1,0:T(8,128)(2,1)}) %reduce-scatter.2.cloned.1.call-update) | async-done | bytes 2293776 | tf_op jit(solution)/shard_map/reduce_scatter | solution.py:55
  244.1 31.4 %all_to_all.39 = bf16[4,80,3584]{2,1,0:T(8,128)(2,1)S(1)} all-to-all(bf16[4,80,3584]{2,1,0:T(8,128)(2,1)} %bitcast.50), channel_id=1, replica_groups=mesh['groups'=2,'dp'=4,'fsdp'=4] {'dp'}, dimensions={0} | all-to-all | bytes 4587520 | tf_op jit(solution)/shard_map/all_to_all | solution.py:56
  275.5 0.0 copy-start.1
  275.5 0.0 copy-start.3
  275.5 0.2 copy.19
  275.7 0.4 pad_dynamic-slice_fusion.1
  276.1 0.5 collective-permute-start.1
  276.6 0.1 copy-done.1
  276.7 0.0 copy-done.3
  276.7 0.5 convolution_convert_fusion.1
  277.2 2.1 concatenate.12
  279.3 28.7 %collective-permute-done.1 = bf16[48,14336]{1,0:T(8,128)(2,1)S(1)} collective-permute-done((bf16[48,14336]{1,0:T(8,128)(2,1)S(1)}, bf16[48,14336]{1,0:T(8,128)(2,1)S(1)}, u32[]{:S(2)}, u32[]{:S(2)}) %collective-permute-start.1) | collective-permute-done | bytes 1376288 | tf_op jit(solution)/shard_map/ppermute | solution.py:12
  308.1 9.0 %dynamic_update_slice.7 = bf16[128,14336]{1,0:T(8,128)(2,1)} dynamic-update-slice(bf16[128,14336]{1,0:T(8,128)(2,1)} %concatenate.12, bf16[48,14336]{1,0:T(8,128)(2,1)S(1)} %collective-permute-done.1, s32[]{:T(128)S(6)} %select_n.16, s32[]{:T(128)} %constant.2.clone.1) | dynamic-update-slice | bytes 2752516 | tf_op jit(solution)/shard_map/dynamic_update_slice | solution.py:29
  317.1 0.0 copy-done
  317.1 8.2 %select_convert_fusion = (bf16[128,14336]{1,0:T(8,128)(2,1)S(1)}, bf16[128,14336]{1,0:T(8,128)(2,1)}) fusion(bf16[128,14336]{1,0:T(8,128)(2,1)} %param.11, bf16[128,14336]{1,0:T(8,128)(2,1)} %dynamic_update_slice.7, pred[128]{0:T(512)(128)(4,1)S(1)} %iota_compare_fusion, bf16[128,32]{0,1:T(8,128)(2,1)S(1)} %convolution_convert_fusion.1, ...), kind=kOutput, calls=%fused_computation.4 | convolution fusion | flops 148635648 | bytes 15605888 | tf_op jit(solution)/shard_map/dot_general | solution.py:62
  325.3 1.8 copy-done.2
  327.1 1.8 fusion
  328.9 4.6 %convolution_bitcast_fusion = f32[1,32,4096]{2,1,0:T(8,128)} fusion(bf16[128,4096]{1,0:T(8,128)(2,1)S(1)} %copy-done.1, bf16[128,14336]{1,0:T(8,128)(2,1)} %copy-done.2, bf16[1,32,14336]{2,1,0:T(8,128)(2,1)S(1)} %copy-done), kind=kOutput, calls=%fused_computation.8 | convolution fusion | flops 151003136 | bytes 6160384 | tf_op jit(solution)/shard_map/dot_general | solution.py:77
  (4 shorter events, 0.1 us)
Async XLA Ops:
  7.2 309.9 %copy-start = (bf16[1,32,14336]{2,1,0:T(8,128)(2,1)S(1)}, bf16[1,32,14336]{2,1,0:T(8,128)(2,1)}, u32[]{:S(2)}) copy-start(bf16[1,32,14336]{2,1,0:T(8,128)(2,1)} %param.9) | copy-start | bytes 2752516
  7.2 62.8 %all-gather.2.cloned.1.call-start = ((), (), s32[]{:S(2)}) async-start(), calls=%async_computation.3 | async-start | bytes 3276800 | tf_op jit(solution)/shard_map/all_gather | solution.py:50
  9.1 12.2 %collective-permute-start = (bf16[48,4096]{1,0:T(8,128)(2,1)S(1)}, bf16[48,4096]{1,0:T(8,128)(2,1)S(1)}, u32[]{:S(2)}, u32[]{:S(2)}) collective-permute-start(bf16[48,4096]{1,0:T(8,128)(2,1)S(1)} %pad_dynamic-slice_fusion), channel_id=1, source_target_pairs={{0,8},{4,12},{8,0},{12,4},{1,9},{5,13},{9,1},{13,5},{2,10},{6,14},... | collective-permute-start | bytes 1179656 | tf_op jit(solution)/shard_map/ppermute | solution.py:12
  44.7 199.4 %reduce-scatter.2.cloned.1.call-start = ((), (), s32[]{:S(2)}) async-start(), calls=%async_computation.4 | async-start | bytes 11468800 | tf_op jit(solution)/shard_map/reduce_scatter | solution.py:55
  275.5 1.2 copy-start.1
  275.5 1.3 copy-start.3
  276.1 31.9 %collective-permute-start.1 = (bf16[48,14336]{1,0:T(8,128)(2,1)S(1)}, bf16[48,14336]{1,0:T(8,128)(2,1)S(1)}, u32[]{:S(2)}, u32[]{:S(2)}) collective-permute-start(bf16[48,14336]{1,0:T(8,128)(2,1)S(1)} %pad_dynamic-slice_fusion.1), channel_id=1, source_target_pairs={{0,8},{4,12},{8,0},{12,4},{1,9},{5,13},{9,1},{13,5},{2,10},{6,14},... | collective-permute-start | bytes 4128776 | tf_op jit(solution)/shard_map/ppermute | solution.py:12
  325.3 1.8 copy-start.2
Sparse Core Ops, SparseCore 0:
  44.8 25.0 all-gather.1
  87.0 157.0 reduce-scatter.1
where the time goes:
time: 341 us; the launch traced here: 340 us
  waiting for transfers between devices  219 us (64%)
  blocking collectives  52.4 us (15%)
  matrix products  30 us (9%)
  local copies, waits for them, and re-layouts  19.3 us (6%)
  between operations  14.8 us (4%)
  starting transfers between devices  3.6 us (1%)
    reduce_scatter x1, waiting for transfers between devices, per_device(): lax.psum_scatter(partial_blocks, 'fsdp', scatter_dimension=0, tiled=True)  157 us
    ppermute x2, waiting for transfers between devices, partner(): lax.ppermute(x, axis, [(i, i ^ 1 << distance) for i in range(lax.axis_siz...  36.5 us
    all_to_all x1, blocking collectives, per_device(): lax.all_to_all(blocks, 'dp', split_axis=0, concat_axis=1, tiled=True)  31.4 us
    all_gather x1, waiting for transfers between devices, per_device(): all_rows = lax.all_gather(sliced_rows, 'dp', axis=0, tiled=True)  25.2 us
    all_to_all x1, blocking collectives, per_device(): lax.all_to_all(paired_rows, 'fsdp', split_axis=1, concat_axis=0, tiled=True)  21 us
    dot_general x1, matrix products, per_device(): jnp.dot(all_rows.reshape(-1, slice_width), up_weight, preferred_element_t...  14.9 us
    dynamic_update_slice x2, local copies, waits for them, and re-layouts, place_block(): placed = lax.dynamic_update_slice_in_dim(padded, block, offset, 0)  11.3 us
    dot_general x1, matrix products, per_device(): jnp.dot(rank_projection, up_factor, preferred_element_type=jnp.float32)  8.18 us
  transfers between devices with their start and end apart: 4, of which 4 were waited for; matrix products, arithmetic and copies ran while one was open for 1% of the time, Pallas kernels for 0%

commit v1 on v0

--- a/solution.py
+++ b/solution.py
@@ -45,7 +45,12 @@
     guest = partner(outgoing, "dp", half_bit)
     paired_rows = place_block(tokens[:PAIR_ROWS], guest, kept_rows, PAIR_ROWS)
     dp_total, fsdp_total = (lax.axis_size("dp"), lax.axis_size("fsdp"))
-    sliced_rows = lax.all_to_all(paired_rows, "fsdp", split_axis=1, concat_axis=0, tiled=True)
+    sliced_rows = jnp.concatenate(
+        lax.all_to_all(
+            jnp.stack(jnp.split(paired_rows, lax.axis_size("fsdp"), axis=1)), "fsdp", 0, 0
+        ),
+        axis=0,
+    )
     slice_width = sliced_rows.shape[1]
     all_rows = lax.all_gather(sliced_rows, "dp", axis=0, tiled=True)
     all_rows = all_rows.reshape(dp_total, fsdp_total, PAIR_ROWS, slice_width).swapaxes(0, 1)

time: 341 us -> 341 us (level)
  no operation moved by 1% of the time
where the time goes in v1:
time: 341 us; the launch traced here: 340 us
  waiting for transfers between devices  219 us (64%)
  blocking collectives  52.4 us (15%)
  matrix products  30 us (9%)
  local copies, waits for them, and re-layouts  19.3 us (6%)
  between operations  14.8 us (4%)
  starting transfers between devices  3.6 us (1%)
    reduce_scatter x1, waiting for transfers between devices, per_device(): lax.psum_scatter(partial_blocks, 'fsdp', scatter_dimension=0, tiled=True)  157 us
    ppermute x2, waiting for transfers between devices, partner(): lax.ppermute(x, axis, [(i, i ^ 1 << distance) for i in range(lax.axis_siz...  36.5 us
    all_to_all x1, blocking collectives, per_device(): lax.all_to_all(blocks, 'dp', split_axis=0, concat_axis=1, tiled=True)  31.4 us
    all_gather x1, waiting for transfers between devices, per_device(): all_rows = lax.all_gather(sliced_rows, 'dp', axis=0, tiled=True)  25.2 us
    all_to_all x1, blocking collectives, per_device(): lax.all_to_all(jnp.stack(jnp.split(paired_rows, lax.axis_size('fsdp'), ax...  21 us
    dot_general x1, matrix products, per_device(): jnp.dot(all_rows.reshape(-1, slice_width), up_weight, preferred_element_t...  14.9 us
    dynamic_update_slice x2, local copies, waits for them, and re-layouts, place_block(): placed = lax.dynamic_update_slice_in_dim(padded, block, offset, 0)  11.3 us
    dot_general x1, matrix products, per_device(): jnp.dot(rank_projection, up_factor, preferred_element_type=jnp.float32)  8.18 us
  transfers between devices with their start and end apart: 4, of which 4 were waited for; matrix products, arithmetic and copies ran while one was open for 1% of the time, Pallas kernels for 0%

profile of v1, /device:TPU:0, one launch (start us, length us, event | category | flops | bytes accessed | tf_op | source)
XLA Modules:
  0.0 340.5 jit_solution(1763433905961873940)
XLA Ops:
  7.2 0.0 copy-start
  7.2 0.0 all-gather.2.cloned.1.call-start
  8.0 1.2 pad_dynamic-slice_fusion
  9.1 3.1 collective-permute-start
  12.2 1.4 broadcast_select_fusion
  13.6 7.7 %collective-permute-done = bf16[48,4096]{1,0:T(8,128)(2,1)S(1)} collective-permute-done((bf16[48,4096]{1,0:T(8,128)(2,1)S(1)}, bf16[48,4096]{1,0:T(8,128)(2,1)S(1)}, u32[]{:S(2)}, u32[]{:S(2)}) %collective-permute-start) | collective-permute-done | bytes 393248 | tf_op jit(solution)/shard_map/ppermute | solution.py:12
  21.3 2.3 dynamic_update_slice.6
  23.6 0.1 pad_maximum_fusion
  23.7 21.0 %all_to_all.24 = bf16[4,80,1024]{2,1,0:T(8,128)(2,1)} all-to-all(bf16[4,80,1024]{2,1,0:T(8,128)(2,1)S(1)} %pad_maximum_fusion), channel_id=1, replica_groups=mesh['groups'=2,'dp'=4,'fsdp'=4] {'fsdp'}, dimensions={0} | all-to-all | bytes 1310720 | tf_op jit(solution)/shard_map/all_to_all | solution.py:49
  44.7 0.0 all-gather.2.cloned.1.call-update
  44.7 0.0 reduce-scatter.2.cloned.1.call-start
  44.8 25.2 %all-gather.2.cloned.1.call-done = bf16[1280,1024]{1,0:T(8,128)(2,1)} async-done(((bf16[320,1024]{1,0:T(8,128)(2,1)}), bf16[1280,1024]{1,0:T(8,128)(2,1)}) %all-gather.2.cloned.1.call-update) | async-done | bytes 2621456 | tf_op jit(solution)/shard_map/all_gather | solution.py:55
  70.0 2.1 copy.11
  72.1 14.9 %convolution_convert_fusion = bf16[1280,3584]{1,0:T(8,128)(2,1)} fusion(bf16[1280,1024]{1,0:T(8,128)(2,1)S(1)} %bitcast.48, bf16[1024,3584]{1,0:T(8,128)(2,1)} %param.7), kind=kOutput, calls=%fused_computation.3 | convolution fusion | flops 9399828480 | bytes 19136512 | tf_op jit(solution)/shard_map/dot_general | solution.py:57
  86.9 0.0 reduce-scatter.2.cloned.1.call-update
  86.9 157.2 %reduce-scatter.2.cloned.1.call-done = bf16[320,3584]{1,0:T(8,128)(2,1)} async-done(((bf16[1280,3584]{1,0:T(8,128)(2,1)}), bf16[320,3584]{1,0:T(8,128)(2,1)}) %reduce-scatter.2.cloned.1.call-update) | async-done | bytes 2293776 | tf_op jit(solution)/shard_map/reduce_scatter | solution.py:60
  244.1 31.4 %all_to_all.25 = bf16[4,80,3584]{2,1,0:T(8,128)(2,1)S(1)} all-to-all(bf16[4,80,3584]{2,1,0:T(8,128)(2,1)} %bitcast.50), channel_id=1, replica_groups=mesh['groups'=2,'dp'=4,'fsdp'=4] {'dp'}, dimensions={0} | all-to-all | bytes 4587520 | tf_op jit(solution)/shard_map/all_to_all | solution.py:61
  275.5 0.0 copy-start.1
  275.5 0.2 copy.13
  275.7 0.4 pad_dynamic-slice_fusion.1
  276.2 0.5 collective-permute-start.1
  276.6 0.1 copy-done.1
  276.7 0.0 copy-done.3
  276.8 0.5 convolution_convert_fusion.1
  277.2 2.1 concatenate.12
  279.4 28.7 %collective-permute-done.1 = bf16[48,14336]{1,0:T(8,128)(2,1)S(1)} collective-permute-done((bf16[48,14336]{1,0:T(8,128)(2,1)S(1)}, bf16[48,14336]{1,0:T(8,128)(2,1)S(1)}, u32[]{:S(2)}, u32[]{:S(2)}) %collective-permute-start.1) | collective-permute-done | bytes 1376288 | tf_op jit(solution)/shard_map/ppermute | solution.py:12
  308.1 9.0 %dynamic_update_slice.7 = bf16[128,14336]{1,0:T(8,128)(2,1)} dynamic-update-slice(bf16[128,14336]{1,0:T(8,128)(2,1)} %concatenate.12, bf16[48,14336]{1,0:T(8,128)(2,1)S(1)} %collective-permute-done.1, s32[]{:T(128)S(6)} %select_n.16, s32[]{:T(128)} %constant.2.clone.1) | dynamic-update-slice | bytes 2752516 | tf_op jit(solution)/shard_map/dynamic_update_slice | solution.py:29
  317.1 0.0 copy-done
  317.1 8.2 %select_convert_fusion = (bf16[128,14336]{1,0:T(8,128)(2,1)S(1)}, bf16[128,14336]{1,0:T(8,128)(2,1)}) fusion(bf16[128,14336]{1,0:T(8,128)(2,1)} %param.11, bf16[128,14336]{1,0:T(8,128)(2,1)} %dynamic_update_slice.7, pred[128]{0:T(512)(128)(4,1)S(1)} %iota_compare_fusion, bf16[128,32]{0,1:T(8,128)(2,1)S(1)} %convolution_convert_fusion.1, ...), kind=kOutput, calls=%fused_computation.4 | convolution fusion | flops 148635648 | bytes 15605888 | tf_op jit(solution)/shard_map/dot_general | solution.py:67
  325.3 1.8 copy-done.2
  327.1 1.8 fusion
  329.0 4.6 %convolution_bitcast_fusion = f32[1,32,4096]{2,1,0:T(8,128)} fusion(bf16[128,4096]{1,0:T(8,128)(2,1)S(1)} %copy-done.1, bf16[128,14336]{1,0:T(8,128)(2,1)} %copy-done.2, bf16[1,32,14336]{2,1,0:T(8,128)(2,1)S(1)} %copy-done), kind=kOutput, calls=%fused_computation.8 | convolution fusion | flops 151003136 | bytes 6160384 | tf_op jit(solution)/shard_map/dot_general | solution.py:82
  (4 shorter events, 0.1 us)
Async XLA Ops:
  7.2 310.0 %copy-start = (bf16[1,32,14336]{2,1,0:T(8,128)(2,1)S(1)}, bf16[1,32,14336]{2,1,0:T(8,128)(2,1)}, u32[]{:S(2)}) copy-start(bf16[1,32,14336]{2,1,0:T(8,128)(2,1)} %param.9) | copy-start | bytes 2752516
  7.2 62.8 %all-gather.2.cloned.1.call-start = ((), (), s32[]{:S(2)}) async-start(), calls=%async_computation.3 | async-start | bytes 3276800 | tf_op jit(solution)/shard_map/all_gather | solution.py:55
  9.1 12.2 %collective-permute-start = (bf16[48,4096]{1,0:T(8,128)(2,1)S(1)}, bf16[48,4096]{1,0:T(8,128)(2,1)S(1)}, u32[]{:S(2)}, u32[]{:S(2)}) collective-permute-start(bf16[48,4096]{1,0:T(8,128)(2,1)S(1)} %pad_dynamic-slice_fusion), channel_id=1, source_target_pairs={{0,8},{4,12},{8,0},{12,4},{1,9},{5,13},{9,1},{13,5},{2,10},{6,14},... | collective-permute-start | bytes 1179656 | tf_op jit(solution)/shard_map/ppermute | solution.py:12
  44.7 199.4 %reduce-scatter.2.cloned.1.call-start = ((), (), s32[]{:S(2)}) async-start(), calls=%async_computation.4 | async-start | bytes 11468800 | tf_op jit(solution)/shard_map/reduce_scatter | solution.py:60
  275.5 1.2 copy-start.1
  275.5 1.3 copy-start.3
  276.2 31.9 %collective-permute-start.1 = (bf16[48,14336]{1,0:T(8,128)(2,1)S(1)}, bf16[48,14336]{1,0:T(8,128)(2,1)S(1)}, u32[]{:S(2)}, u32[]{:S(2)}) collective-permute-start(bf16[48,14336]{1,0:T(8,128)(2,1)S(1)} %pad_dynamic-slice_fusion.1), channel_id=1, source_target_pairs={{0,8},{4,12},{8,0},{12,4},{1,9},{5,13},{9,1},{13,5},{2,10},{6,14},... | collective-permute-start | bytes 4128776 | tf_op jit(solution)/shard_map/ppermute | solution.py:12
  325.3 1.8 copy-start.2
Sparse Core Ops, SparseCore 0:
  44.9 25.0 all-gather.1
  87.1 157.0 reduce-scatter.1
